TPU v7x, 32 devices: a whole 2x2x4 slice. The times are simulated.
32 devices in a mesh: dp: 1, tp: 32 (over x, y, z, core).
Axes of the slice: x: 2, y: 2, z: 4, core: 2. Of those that a mesh axis runs over, the one named last changes fastest.
Arguments:
- x: bfloat16 [128, 12288], P('dp')
- w_gate: bfloat16 [12288, 28672], P(None, 'tp')
- w_up: bfloat16 [12288, 28672], P(None, 'tp')
- w_down: bfloat16 [28672, 12288], P('tp')
Outputs:
- output: bfloat16 [128, 12288], P('dp')
All inputs are finite; a program needn't handle non-finite values.
Results may differ from a plain program's by a relative error of at most 0.016.
Values are sent between devices in bfloat16 or wider.
A program may use at most 2 GiB of HBM per device.

v0:
```python
import jax
import jax.numpy as jnp
from jax import lax
from jax.sharding import PartitionSpec as P


def solution(mesh):
    def step(x, w_gate, w_up, w_down):
        gate = jnp.dot(x, w_gate, preferred_element_type=jnp.float32)
        up = jnp.dot(x, w_up, preferred_element_type=jnp.float32)
        hidden = (jax.nn.silu(gate) * up).astype(jnp.bfloat16)
        term = jnp.dot(hidden, w_down, preferred_element_type=jnp.float32).astype(jnp.bfloat16)
        return lax.psum(term, "tp")

    return jax.shard_map(
        step,
        mesh=mesh,
        in_specs=(P("dp", None), P(None, "tp"), P(None, "tp"), P("tp", None)),
        out_specs=P("dp", None),
        check_vma=False,
    )
```

profile of v0, /device:TPU:0, one launch (start us, length us, event | category | flops | bytes accessed | tf_op | source)
XLA Modules:
  0.0 191.0 jit_solution(14570245020826880759)
XLA Ops:
  6.5 0.0 copy-start
  6.5 0.0 all-reduce.2.cloned.1.call-start
  6.5 1.9 copy-done
  8.4 9.8 %fusion.1 = f32[128,896]{1,0:T(8,128)} fusion(bf16[128,12288]{1,0:T(8,128)(2,1)S(1)} %copy-done, bf16[12288,896]{1,0:T(8,128)(2,1)} %param.5), kind=kOutput, calls=%fused_computation.3 | convolution fusion | flops 2818572288 | bytes 25624576 | tf_op jit(solution)/shard_map/dot_general | solution.py:9
  18.3 21.9 %convolution_convert_fusion = bf16[128,12288]{1,0:T(8,128)(2,1)} fusion(bf16[896,12288]{1,0:T(8,128)(2,1)} %param.7, bf16[128,12288]{1,0:T(8,128)(2,1)S(1)} %copy-done, bf16[12288,896]{1,0:T(8,128)(2,1)} %param.6, f32[128,896]{1,0:T(8,128)} %fusion.1), kind=kOutput, calls=%fused_computation | convolution fusion | flops 5639405568 | bytes 50790400 | tf_op jit(solution)/shard_map/dot_general | solution.py:12
  40.2 0.0 all-reduce.2.cloned.1.call-update
  40.2 140.2 %all-reduce.2.cloned.1.call-done = bf16[128,12288]{1,0:T(8,128)(2,1)} async-done(((bf16[128,12288]{1,0:T(8,128)(2,1)}), bf16[128,12288]{1,0:T(8,128)(2,1)}) %all-reduce.2.cloned.1.call-update) | async-done | bytes 3145744 | tf_op jit(solution)/shard_map/psum | solution.py:13
  180.4 3.8 %copy.6 = bf16[128,12288]{1,0:T(8,128)(2,1)} copy(bf16[128,12288]{1,0:T(8,128)(2,1)} %all-reduce.2.cloned.1.call-done) | data formatting | bytes 6291456
Async XLA Ops:
  6.5 1.9 copy-start
  6.5 173.8 %all-reduce.2.cloned.1.call-start = ((), (), s32[]{:S(2)}) async-start(), calls=%async_computation | async-start | bytes 6291456 | tf_op jit(solution)/shard_map/psum | solution.py:13
Sparse Core Ops, SparseCore 0:
  40.3 139.9 all-reduce.1
where the time goes:
time: 191 us
  waiting for transfers between devices  140 us (73%)
  matrix products  31.8 us (17%)
  between operations  13.4 us (7%)
  local copies, waits for them, and re-layouts  5.72 us (3%)
    psum x1, waiting for transfers between devices, step(): return lax.psum(term, 'tp')  140 us
    dot_general x1, matrix products, step(): jnp.dot(hidden, w_down, preferred_element_type=jnp.float32)  21.9 us
    dot_general x1, matrix products, step(): gate = jnp.dot(x, w_gate, preferred_element_type=jnp.float32)  9.83 us
    unnamed x3, local copies, waits for them, and re-layouts  5.72 us
  transfers between devices with their start and end apart: 1, of which 1 were waited for; matrix products, arithmetic and copies ran while one was open for 0% of the time, Pallas kernels for 0%

commit v1 on v0

v1 whole, which is shorter than its diff:
```python
import functools

import jax
import jax.numpy as jnp
from jax import lax
from jax.experimental import pallas as pl
from jax.experimental.pallas import tpu as pltpu
from jax.sharding import PartitionSpec as P

ROWS, D, FF = 128, 12288, 896
BLK = 8
NB = ROWS // BLK
R = 512
STEPS = D // R
NS = 8
K = 4
HALF = D // 2
W = HALF // K
WH = W // 2
S = 2 * K
F32, BF16 = jnp.float32, jnp.bfloat16
MESH = pl.DeviceIdType.MESH


def kernel(
    x_hbm, wg_hbm, wu_hbm, wd_hbm, y_hbm,
    wbuf, xbuf, acc, hid, wd, own, d_send, d_recv, s1, r1, s2, r2, s3, r3, yv,
    psem, wsem, osem,
    d_ss, d_rs, s1_ss, s1_rs, s2_ss, s2_rs, s3_ss, s3_rs,
    g3_ss, g3_rs, g2_ss, g2_rs, g1_ss, g1_rs, h_ss, h_rs,
):
    me = lax.axis_index("tp")
    core = lax.rem(me, 2)
    z = lax.rem(lax.div(me, 2), 4)
    y = lax.rem(lax.div(me, 8), 2)
    x = lax.div(me, 16)
    partner = me + 1 - 2 * core
    nbr = (me + 16 * (1 - 2 * x), me + 8 * (1 - 2 * y))
    zpos = [lax.rem(z + j, 4) for j in (1, 2, 3)]
    zpeer = [me + 2 * (q - z) for q in zpos]
    coord = (x, y)

    barrier = pltpu.get_barrier_semaphore()
    for peer in (partner, *nbr, *zpeer):
        pl.semaphore_signal(barrier, inc=1, device_id={"tp": peer}, device_id_type=MESH)

    def stream(step, slot):
        rows = pl.ds(pl.multiple_of(step * R, R), R)
        return (
            pltpu.make_async_copy(wg_hbm.at[rows, :], wbuf.at[slot, :, pl.ds(0, FF)], psem.at[0, slot]),
            pltpu.make_async_copy(wu_hbm.at[rows, :], wbuf.at[slot, :, pl.ds(FF, FF)], psem.at[1, slot]),
            pltpu.make_async_copy(x_hbm.at[:, rows], xbuf.at[slot], psem.at[2, slot]),
        )

    def down(t):
        odd = lax.rem(t, 2)
        half = odd * core + (1 - odd) * (1 - core)
        cols = pl.ds(pl.multiple_of(half * HALF + lax.div(t, 2) * W, W), W)
        return pltpu.make_async_copy(wd_hbm.at[:, cols], wd.at[t], wsem.at[t])

    def project(step):
        slot = lax.rem(step, NS)
        for c in stream(step, slot):
            c.wait()
        acc[...] += jnp.dot(xbuf[slot], wbuf[slot], preferred_element_type=F32)
        return slot

    for i in range(NS):
        for c in stream(i, i):
            c.start()
    acc[...] = jnp.zeros_like(acc)

    @pl.loop(0, STEPS - NS)
    def _(step):
        slot = project(step)
        for c in stream(step + NS, slot):
            c.start()

    @pl.loop(STEPS - NS, STEPS)
    def _(step):
        down(step - (STEPS - NS)).start()
        project(step)

    gate, up = acc[:, :FF], acc[:, FF:]
    hid[...] = (jax.nn.silu(gate) * up).astype(BF16)
    pl.semaphore_wait(barrier, 6)

    def remote(src, dst, ss, rs, peer):
        return pltpu.make_async_remote_copy(
            src_ref=src, dst_ref=dst, send_sem=ss, recv_sem=rs, device_id={"tp": peer}, device_id_type=MESH
        )

    def ab(s):
        i = s % 2
        return coord[i], coord[1 - i], nbr[i], nbr[1 - i]

    def mine(s):
        return core * S + s

    def d_copy(s):
        return remote(d_send.at[s], d_recv.at[s], d_ss.at[s], d_rs.at[s], partner)

    def s1_copy(s):
        return remote(s1.at[s], r1.at[s], s1_ss.at[s], s1_rs.at[s], ab(s)[2])

    def s2_copy(s):
        return remote(s2.at[s], r2.at[s], s2_ss.at[s], s2_rs.at[s], ab(s)[3])

    def s3_copy(s, j):
        return remote(s3.at[s, j], r3.at[s, j], s3_ss.at[s, j], s3_rs.at[s, j], zpeer[j])

    def g3_copy(s, j):
        a, b, _, _ = ab(s)
        ref = yv.at[mine(s), 8 * a + 4 * b + z]
        return remote(ref, ref, g3_ss.at[s, j], g3_rs.at[s, j], zpeer[j])

    def g2_copy(s):
        a, b, _, peer = ab(s)
        ref = yv.at[mine(s), pl.ds(8 * a + 4 * b, 4)]
        return remote(ref, ref, g2_ss.at[s], g2_rs.at[s], peer)

    def g1_copy(s):
        a, _, peer, _ = ab(s)
        ref = yv.at[mine(s), pl.ds(8 * a, 8)]
        return remote(ref, ref, g1_ss.at[s], g1_rs.at[s], peer)

    def h_copy(s, i):
        a = ab(s)[0]
        ref = yv.at[mine(s), pl.ds(8 * a if i == 0 else 8 * (1 - a), 8)]
        return remote(ref, ref, h_ss.at[s, i], h_rs.at[s, i], partner)

    def out_copy(g, i):
        return pltpu.make_async_copy(yv.at[g], y_hbm.at[:, :, pl.ds(pl.multiple_of(g * WH, WH), WH)], osem.at[i])

    def subs(k):
        return (2 * k, 2 * k + 1)

    def compute(k):
        for t in (2 * k, 2 * k + 1):
            down(t).wait()
            for i, s in enumerate(subs(k)):
                p = jnp.dot(hid[...], wd[t, :, i * WH : (i + 1) * WH], preferred_element_type=F32)
                p = p.reshape(NB, BLK, WH)
                if t % 2 == 0:
                    d_send[s] = p.astype(BF16)
                    d_copy(s).start()
                else:
                    own[s] = p

    def first(k):
        for s in subs(k):
            a = ab(s)[0]
            d_copy(s).wait_recv()
            go, keep = pl.ds(8 * (1 - a), 8), pl.ds(8 * a, 8)
            s1[s] = (own[s, go] + d_recv[s, go].astype(F32)).astype(BF16)
            s1_copy(s).start()
            own[s, keep] += d_recv[s, keep].astype(F32)

    def second(k):
        for s in subs(k):
            a, b, _, _ = ab(s)
            s1_copy(s).wait_recv()
            go, keep = 4 * (1 - b), 4 * b
            s2[s] = (own[s, pl.ds(8 * a + go, 4)] + r1[s, pl.ds(go, 4)].astype(F32)).astype(BF16)
            s2_copy(s).start()
            own[s, pl.ds(8 * a + keep, 4)] += r1[s, pl.ds(keep, 4)].astype(F32)

    def third(k):
        for s in subs(k):
            a, b, _, _ = ab(s)
            s2_copy(s).wait_recv()
            base = 8 * a + 4 * b
            for j in range(3):
                q = zpos[j]
                s3[s, j] = (own[s, base + q] + r2[s, q].astype(F32)).astype(BF16)
                s3_copy(s, j).start()

    def final(k):
        for s in subs(k):
            a, b, _, _ = ab(s)
            base = 8 * a + 4 * b
            total = own[s, base + z] + r2[s, z].astype(F32)
            for j in range(3):
                s3_copy(s, j).wait_recv()
                total += r3[s, j].astype(F32)
            yv[mine(s), base + z] = total.astype(BF16)
            for j in range(3):
                g3_copy(s, j).start()

    def gather_b(k):
        for s in subs(k):
            for j in range(3):
                g3_copy(s, j).wait_recv()
            g2_copy(s).start()

    def gather_a(k):
        for s in subs(k):
            g2_copy(s).wait_recv()
            g1_copy(s).start()
            h_copy(s, 0).start()

    def gather_core(k):
        for s in subs(k):
            g1_copy(s).wait_recv()
            h_copy(s, 1).start()
            out_copy(mine(s), s).start()

    def finish(k):
        for s in subs(k):
            h_copy(s, 0).wait_recv()
            h_copy(s, 1).wait_recv()
            out_copy((1 - core) * S + s, S + s).start()

    stages = (compute, first, second, third, final, gather_b, gather_a, gather_core, finish)
    for time in range(K + len(stages) - 1):
        for i, stage in enumerate(stages):
            if 0 <= time - i < K:
                stage(time - i)

    for s in range(S):
        d_copy(s).wait_send()
        s1_copy(s).wait_send()
        s2_copy(s).wait_send()
        g2_copy(s).wait_send()
        g1_copy(s).wait_send()
        for j in range(3):
            s3_copy(s, j).wait_send()
            g3_copy(s, j).wait_send()
        for i in range(2):
            h_copy(s, i).wait_send()
        out_copy(mine(s), s).wait()
        out_copy((1 - core) * S + s, S + s).wait()


def block(x, w_gate, w_up, w_down):
    dma = pltpu.SemaphoreType.DMA
    out = pl.pallas_call(
        kernel,
        name="mlp",
        out_shape=jax.ShapeDtypeStruct((NB, BLK, D), BF16),
        in_specs=[pl.BlockSpec(memory_space=pl.ANY)] * 4,
        out_specs=pl.BlockSpec(memory_space=pl.ANY),
        scratch_shapes=[
            pltpu.VMEM((NS, R, 2 * FF), BF16),
            pltpu.VMEM((NS, ROWS, R), BF16),
            pltpu.VMEM((ROWS, 2 * FF), F32),
            pltpu.VMEM((ROWS, FF), BF16),
            pltpu.VMEM((2 * K, FF, W), BF16),
            pltpu.VMEM((S, NB, BLK, WH), F32),
            pltpu.VMEM((S, NB, BLK, WH), BF16),
            pltpu.VMEM((S, NB, BLK, WH), BF16),
            pltpu.VMEM((S, 8, BLK, WH), BF16),
            pltpu.VMEM((S, 8, BLK, WH), BF16),
            pltpu.VMEM((S, 4, BLK, WH), BF16),
            pltpu.VMEM((S, 4, BLK, WH), BF16),
            pltpu.VMEM((S, 3, BLK, WH), BF16),
            pltpu.VMEM((S, 3, BLK, WH), BF16),
            pltpu.VMEM((2 * S, NB, BLK, WH), BF16),
            dma((3, NS)),
            dma((2 * K,)),
            dma((2 * S,)),
            *[dma((S,))] * 6,
            *[dma((S, 3))] * 4,
            *[dma((S,))] * 4,
            *[dma((S, 2))] * 2,
        ],
        compiler_params=pltpu.CompilerParams(
            collective_id=0, has_side_effects=True, vmem_limit_bytes=63 * 1024 * 1024
        ),
        cost_estimate=pl.CostEstimate(flops=6 * ROWS * D * FF, bytes_accessed=6 * D * FF, transcendentals=ROWS * FF),
    )(x, w_gate, w_up, w_down)
    return out.reshape(ROWS, D)


def solution(mesh):
    return jax.shard_map(
        block,
        mesh=mesh,
        in_specs=(P("dp", None), P(None, "tp"), P(None, "tp"), P("tp", None)),
        out_specs=P("dp", None),
        check_vma=False,
    )
```

time: 191 us -> 66.1 us (0.35)
  waiting for transfers between devices: 140 us -> 0 us
  Pallas kernels: 0 us -> 61.5 us
  matrix products: 31.8 us -> 0 us
  between operations: 13.4 us -> 0.01 us
    psum x1 -> x0, waiting for transfers between devices: 140 us -> none  [step(): return lax.psum(term, 'tp')]
    pallas_call x0 -> x1, Pallas kernels: none -> 61.5 us  [block(): pl.pallas_call(kernel, name='mlp', out_shape=jax.ShapeDtypeStruct((NB, BL...]
    dot_general x2 -> x0, matrix products: 31.8 us -> none  [the longest x1 21.9 us: step(): jnp.dot(hidden, w_down, preferred_element_type=jnp.float32)]
    unnamed x3 -> x1, local copies, waits for them, and re-layouts: 5.72 us -> 3.83 us
  transfers between devices with their start and end apart: 1 -> 0, of which waited for: 1 -> 0; matrix products, arithmetic and copies ran while one was open for 0% -> 0% of each run, Pallas kernels for 0% -> 0%
where the time goes in v1:
time: 66.1 us; the launch traced here: 65.4 us
  Pallas kernels  61.5 us (93%)
  local copies, waits for them, and re-layouts  3.83 us (6%)
    pallas_call x1, Pallas kernels, block(): pl.pallas_call(kernel, name='mlp', out_shape=jax.ShapeDtypeStruct((NB, BL...  61.5 us
    unnamed x1, local copies, waits for them, and re-layouts  3.83 us

profile of v1, /device:TPU:0, one launch (start us, length us, event | category | flops | bytes accessed | tf_op | source)
XLA Modules:
  0.0 65.4 jit_solution(17499818510279495589)
XLA Ops:
  0.0 61.5 %mlp.1 = bf16[16,8,12288]{2,1,0:T(8,128)(2,1)} custom-call(bf16[128,12288]{1,0:T(8,128)(2,1)} %x_hbm.1, bf16[12288,896]{1,0:T(8,128)(2,1)} %wg_hbm.1, bf16[12288,896]{1,0:T(8,128)(2,1)} %wu_hbm.1, bf16[896,12288]{1,0:T(8,128)(2,1)} %wd_hbm.1), custom_call_target="tpu_custom_call" | custom-call | flops 8455716864 | bytes 66060288 | tf_op jit(solution)/shard_map/mlp/pallas_call | solution.py:237
  61.5 3.8 %copy.6 = bf16[128,12288]{1,0:T(8,128)(2,1)} copy(bf16[128,12288]{1,0:T(8,128)(2,1)} %bitcast.1) | data formatting | bytes 6291456

commit v2 on v0

v2 whole, which is shorter than its diff:
```python
import jax
import jax.numpy as jnp
from jax import lax
from jax.experimental import pallas as pl
from jax.experimental.pallas import tpu as pltpu
from jax.sharding import PartitionSpec as P

ROWS, D, FF = 128, 12288, 896
BLK = 8
NB = ROWS // BLK
R = 512
STEPS = D // R
NS = 8
HALF = D // 2
T = 512
TILES = 2 * HALF // T
PER = TILES // NS
CHUNKS = (
    (1024, "nfyx"), (512, "xyq"), (512, "yxq"), (512, "nfxy"), (512, "xyq"), (512, "yxq"), (768, "yxq"),
    (512, "nfyx"), (768, "xyq"), (512, "yxq"),
)
ORDER = (
    0, 1, 2, 3, 0, 4, 1, 5, 2, 3, 6, 4, 7, 5, 8, 6, 9, 1, 7, 2, 0, 8, 4, 9, 5, 3, 2, 7, 6, 1, 8, 4, 0, 5, 3, 9, 6,
    7, 2, 8, 3, 0, 1, 9, 4, 7, 5, 3, 0, 6, 7, 2, 3, 8, 0, 1, 7, 9, 2, 3, 4, 0, 5, 1, 7, 6, 8, 2, 5, 3, 9, 4, 2, 1,
    0, 7, 8, 6, 1, 9, 3, 5, 4, 3, 5, 4, 0, 6, 8, 0, 7, 6, 9, 8, 7, 9,
)
S = len(CHUNKS)
STARTS = [sum(w for w, _ in CHUNKS[:s]) for s in range(S)]
F32, BF16 = jnp.float32, jnp.bfloat16
MESH = pl.DeviceIdType.MESH


def kernel(
    x_hbm, wg_hbm, wu_hbm, wd_hbm, out,
    wbuf, xbuf, acc, hid, wd, own, sbuf, rbuf,
    psem, wsem, send_sem, recv_sem, send_core, recv_core,
):
    me = lax.axis_index("tp")
    core = lax.rem(me, 2)
    z = lax.rem(lax.div(me, 2), 4)
    y = lax.rem(lax.div(me, 8), 2)
    x = lax.div(me, 16)
    near, far = lax.rem(z, 2), lax.div(z, 2)
    partner = me + 1 - 2 * core
    step_n, step_f = 2 * (1 - 2 * near), 4 * (1 - 2 * far)
    bit = {"x": x, "y": y, "n": near, "f": far}
    peer = {"x": me + 16 * (1 - 2 * x), "y": me + 8 * (1 - 2 * y), "n": me + step_n, "f": me + step_f}
    flip_n, flip_f = 1 - near, 1 - far
    others = (
        (2 * far + flip_n, me + step_n),
        (2 * flip_f + near, me + step_f),
        (2 * flip_f + flip_n, me + step_n + step_f),
    )

    barrier = pltpu.get_barrier_semaphore()
    for device in (partner, peer["x"], peer["y"], *[device for _, device in others]):
        pl.semaphore_signal(barrier, inc=1, device_id={"tp": device}, device_id_type=MESH)

    def stream(step, slot):
        rows = pl.ds(pl.multiple_of(step * R, R), R)
        return (
            pltpu.make_async_copy(wg_hbm.at[rows, :], wbuf.at[slot, :, pl.ds(0, FF)], psem.at[0, slot]),
            pltpu.make_async_copy(wu_hbm.at[rows, :], wbuf.at[slot, :, pl.ds(FF, FF)], psem.at[1, slot]),
            pltpu.make_async_copy(x_hbm.at[:, rows], xbuf.at[slot], psem.at[2, slot]),
        )

    def down(t):
        odd = lax.rem(t, 2)
        half = odd * core + (1 - odd) * (1 - core)
        inner = lax.div(t, 2) * T
        src = wd_hbm.at[:, pl.ds(pl.multiple_of(half * HALF + inner, T), T)]
        return pltpu.make_async_copy(src, wd.at[odd, :, pl.ds(pl.multiple_of(inner, T), T)], wsem.at[t])

    def project(step):
        slot = lax.rem(step, NS)
        for c in stream(step, slot):
            c.wait()
        acc[...] += jnp.dot(xbuf[slot], wbuf[slot], preferred_element_type=F32)
        return slot

    for i in range(NS):
        for c in stream(i, i):
            c.start()
    acc[...] = jnp.zeros_like(acc)

    @pl.loop(0, STEPS - NS)
    def _(step):
        slot = project(step)
        for c in stream(step + NS, slot):
            c.start()

    @pl.loop(STEPS - NS, STEPS)
    def _(step):
        for i in range(PER):
            down(PER * (step - (STEPS - NS)) + i).start()
        project(step)

    gate, up = acc[:, :FF], acc[:, FF:]
    hid[...] = (jax.nn.silu(gate) * up).astype(BF16)
    pl.semaphore_wait(barrier, 6)

    def remote(src, dst, ss, rs, device):
        return pltpu.make_async_remote_copy(
            src_ref=src, dst_ref=dst, send_sem=ss, recv_sem=rs, device_id={"tp": device}, device_id_type=MESH
        )

    waited = set()

    def chunk(s):
        width, dims = CHUNKS[s]
        start, m = STARTS[s], len(dims)
        cols = pl.ds(start, width)
        ocols = pl.ds(pl.multiple_of(core * HALF + start, 256), width)
        pcols = pl.ds(pl.multiple_of((1 - core) * HALF + start, 256), width)
        at, sizes = [0], [NB]
        for d in dims:
            if d == "q":
                at.append(at[-1] + 2 * far + near)
                sizes.append(1)
            else:
                sizes.append(sizes[-1] // 2)
                at.append(at[-1] + bit[d] * sizes[-1])
        sends = []

        def go(j):
            return at[j] + (1 - bit[dims[j]]) * sizes[j + 1]

        def place(j):
            return 2 * NB - 2 * sizes[j + 1] if dims[j] != "q" else 28

        def rs(j):
            if dims[j] == "q":
                return [
                    remote(sbuf.at[28 + i, :, cols], rbuf.at[28 + i, :, cols], send_sem.at[s, j], recv_sem.at[s, j], device)
                    for i, (_, device) in enumerate(others)
                ]
            span = pl.ds(place(j), sizes[j + 1])
            ref = (sbuf.at[span, :, cols], rbuf.at[span, :, cols])
            return [remote(*ref, send_sem.at[s, j], recv_sem.at[s, j], peer[dims[j]])]

        def ag(j):
            span = pl.ds(at[j + 1], sizes[j + 1])
            ref = out.at[span, :, ocols]
            devices = [device for _, device in others] if dims[j] == "q" else [peer[dims[j]]]
            return [remote(ref, ref, send_sem.at[s, 4 + j], recv_sem.at[s, 4 + j], device) for device in devices]

        def core_sum():
            span = pl.ds(0, NB)
            return remote(sbuf.at[span, :, cols], rbuf.at[span, :, cols], send_core.at[s, 0], recv_core.at[s, 0], partner)

        def core_gather(i):
            span = pl.ds(at[1] if i == 0 else go(0), NB // 2)
            ref = out.at[span, :, ocols]
            return remote(ref, ref, send_core.at[s, 1 + i], recv_core.at[s, 1 + i], partner)

        def start_all(copies):
            for c in copies:
                c.start()

        def three(sem):
            ref = rbuf.at[pl.ds(28, 3), :, cols]
            pltpu.make_async_copy(ref, ref, sem).wait()

        def arrived(copies, j, sem):
            if dims[j] == "q":
                three(sem)
            else:
                copies(j)[0].wait_recv()

        def drain():
            core_sum().wait_send()
            for i in range(2):
                core_gather(i).wait_send()
            for j in range(m):
                for copies, sem in ((rs, send_sem.at[s, j]), (ag, send_sem.at[s, 4 + j])):
                    if dims[j] == "q":
                        three(sem)
                    else:
                        copies(j)[0].wait_send()

        def matmul():
            for side in (0, 1):
                for t in range(2 * (start // T) + side, 2 * ((start + width - 1) // T) + side + 1, 2):
                    if t not in waited:
                        waited.add(t)
                        down(t).wait()
                p = jnp.dot(hid[...], wd[side, :, cols], preferred_element_type=F32).reshape(NB, BLK, width)
                if side == 0:
                    sbuf[pl.ds(0, NB), :, cols] = p.astype(BF16)
                    core_sum().start()
                else:
                    own[:, :, cols] = p

        yield matmul
        for j in range(m):

            def reduce(j=j):
                if j == 0:
                    core_sum().wait_recv()
                    seen = 0
                else:
                    arrived(rs, j - 1, recv_sem.at[s, j - 1])
                    seen = place(j - 1)

                def total(first, count):
                    got = rbuf[pl.ds(seen + first - at[j], count), :, cols]
                    return own[pl.ds(first, count), :, cols] + got.astype(F32)

                if dims[j] == "q":
                    for i, (q, _) in enumerate(others):
                        sbuf[pl.ds(28 + i, 1), :, cols] = total(at[j] + q, 1).astype(BF16)
                    start_all(rs(j))
                else:
                    sbuf[pl.ds(place(j), sizes[j + 1]), :, cols] = total(go(j), sizes[j + 1]).astype(BF16)
                    start_all(rs(j))
                own[pl.ds(at[j + 1], sizes[j + 1]), :, cols] = total(at[j + 1], sizes[j + 1])

            yield reduce

        def finish():
            arrived(rs, m - 1, recv_sem.at[s, m - 1])
            count = 3 if dims[-1] == "q" else 1
            total = own[pl.ds(at[m], 1), :, cols]
            for i in range(count):
                total += rbuf[pl.ds(place(m - 1) + i, 1), :, cols].astype(F32)
            out[pl.ds(at[m], 1), :, ocols] = total.astype(BF16)
            start_all(ag(m - 1))

        yield finish
        for j in range(m - 2, -1, -1):

            def gather(j=j):
                arrived(ag, j + 1, recv_sem.at[s, 4 + j + 1])
                start_all(ag(j))
                if j == 0:
                    core_gather(0).start()

            yield gather

        def gather_core():
            arrived(ag, 0, recv_sem.at[s, 4])
            core_gather(1).start()

        yield gather_core

        def done():
            core_gather(0).wait_recv()
            core_gather(1).wait_recv()
            drain()

        yield done

    chunks = [chunk(s) for s in range(S)]
    for s in ORDER:
        task = next(chunks[s])
        with jax.named_scope(f"{task.__name__}_{s}"):
            task()


def block(x, w_gate, w_up, w_down):
    dma = pltpu.SemaphoreType.DMA
    out = pl.pallas_call(
        kernel,
        name="mlp",
        out_shape=pltpu.VMEM((NB, BLK, D), BF16),
        in_specs=[pl.BlockSpec(memory_space=pl.ANY)] * 4,
        out_specs=pl.BlockSpec(memory_space=pltpu.VMEM),
        scratch_shapes=[
            pltpu.VMEM((NS, R, 2 * FF), BF16),
            pltpu.VMEM((NS, ROWS, R), BF16),
            pltpu.VMEM((ROWS, 2 * FF), F32),
            pltpu.VMEM((ROWS, FF), BF16),
            pltpu.VMEM((2, FF, HALF), BF16),
            pltpu.VMEM((NB, BLK, HALF), F32),
            pltpu.VMEM((2 * NB, BLK, HALF), BF16),
            pltpu.VMEM((2 * NB, BLK, HALF), BF16),
            dma((3, NS)),
            dma((TILES,)),
            dma((S, 8)),
            dma((S, 8)),
            dma((S, 3)),
            dma((S, 3)),
        ],
        compiler_params=pltpu.CompilerParams(
            collective_id=0, has_side_effects=True, vmem_limit_bytes=58 * 1024 * 1024
        ),
        cost_estimate=pl.CostEstimate(flops=6 * ROWS * D * FF, bytes_accessed=6 * D * FF, transcendentals=ROWS * FF),
    )(x, w_gate, w_up, w_down)
    return out.reshape(ROWS, D)


def solution(mesh):
    return jax.shard_map(
        block,
        mesh=mesh,
        in_specs=(P("dp", None), P(None, "tp"), P(None, "tp"), P("tp", None)),
        out_specs=P("dp", None),
        check_vma=False,
    )
```

time: 191 us -> 63.4 us (0.33)
  waiting for transfers between devices: 140 us -> 0 us
  Pallas kernels: 0 us -> 61.6 us
  matrix products: 31.8 us -> 0 us
  between operations: 13.4 us -> 0.01 us
  local copies, waits for them, and re-layouts: 5.72 us -> 1.67 us
    psum x1 -> x0, waiting for transfers between devices: 140 us -> none  [step(): return lax.psum(term, 'tp')]
    pallas_call x0 -> x1, Pallas kernels: none -> 61.6 us  [block(): pl.pallas_call(kernel, name='mlp', out_shape=pltpu.VMEM((NB, BLK, D), BF1...]
    dot_general x2 -> x0, matrix products: 31.8 us -> none  [the longest x1 21.9 us: step(): jnp.dot(hidden, w_down, preferred_element_type=jnp.float32)]
    unnamed x3 -> x1, local copies, waits for them, and re-layouts: 5.72 us -> 1.67 us
  transfers between devices with their start and end apart: 1 -> 0, of which waited for: 1 -> 0; matrix products, arithmetic and copies ran while one was open for 0% -> 0% of each run, Pallas kernels for 0% -> 0%
where the time goes in v2:
time: 63.4 us; the launch traced here: 63.2 us
  Pallas kernels  61.6 us (97%)
  local copies, waits for them, and re-layouts  1.67 us (3%)
    pallas_call x1, Pallas kernels, block(): pl.pallas_call(kernel, name='mlp', out_shape=pltpu.VMEM((NB, BLK, D), BF1...  61.6 us
    unnamed x1, local copies, waits for them, and re-layouts  1.67 us

profile of v2, /device:TPU:0, one launch (start us, length us, event | category | flops | bytes accessed | tf_op | source)
XLA Modules:
  0.0 63.2 jit_solution(10253156018776339335)
XLA Ops:
  0.0 61.6 %mlp.1 = bf16[16,8,12288]{2,1,0:T(8,128)(2,1)S(1)} custom-call(bf16[128,12288]{1,0:T(8,128)(2,1)} %x_hbm.1, bf16[12288,896]{1,0:T(8,128)(2,1)} %wg_hbm.1, bf16[12288,896]{1,0:T(8,128)(2,1)} %wu_hbm.1, bf16[896,12288]{1,0:T(8,128)(2,1)} %wd_hbm.1), custom_call_target="tpu_custom_call" | custom-call | flops 8455716864 | bytes 66060288 | tf_op jit(solution)/shard_map/mlp/pallas_call | solution.py:262
  61.6 1.7 %copy.6 = bf16[128,12288]{1,0:T(8,128)(2,1)} copy(bf16[128,12288]{1,0:T(8,128)(2,1)S(1)} %bitcast.1) | data formatting | bytes 6291456

commit v3 on v2

v3 whole, which is shorter than its diff:
```python
import jax
import jax.numpy as jnp
from jax import lax
from jax.experimental import pallas as pl
from jax.experimental.pallas import tpu as pltpu
from jax.sharding import PartitionSpec as P

ROWS, D, FF = 128, 12288, 896
BLK = 8
NB = ROWS // BLK
R = 512
STEPS = D // R
NS = 4
HALF = D // 2
T = 1536
TILES = 2 * HALF // T
PER = TILES // NS
CHUNKS = (
    (768, "pq"), (768, "nfyX"), (768, "pq"), (256, "pq"), (768, "yxq"), (512, "nfxY"), (768, "xyq"), (768, "yxq"),
    (768, "xyq"),
)
ORDER = (
    0, 1, 0, 2, 1, 5, 2, 3, 6, 5, 4, 1, 3, 8, 6, 0, 7, 4, 2, 8, 5, 3, 6, 7, 0, 1, 4, 6, 2, 7, 8, 5, 4, 1, 3, 7, 8,
    5, 0, 6, 4, 1, 3, 8, 2, 7, 5, 3, 1, 4, 6, 8, 2, 5, 7, 4, 6, 1, 7, 8, 3, 0, 5, 2, 4, 1, 6, 4, 7, 0, 5, 6, 1, 8,
    5, 7, 8,
)
S = len(CHUNKS)
STARTS = [sum(w for w, _ in CHUNKS[:s]) for s in range(S)]
F32, BF16 = jnp.float32, jnp.bfloat16
MESH = pl.DeviceIdType.MESH


def kernel(
    x_hbm, wg_hbm, wu_hbm, wd_hbm, out,
    wbuf, xbuf, acc, hid, wd, own, sbuf, rbuf, swap,
    psem, wsem, send_rs, send_ag, send_swap, recv_sem,
):
    me = lax.axis_index("tp")
    core = lax.rem(me, 2)
    z = lax.rem(lax.div(me, 2), 4)
    y = lax.rem(lax.div(me, 8), 2)
    x = lax.div(me, 16)
    near, far = lax.rem(z, 2), lax.div(z, 2)
    partner = me + 1 - 2 * core
    bit = {"x": x, "y": y, "n": near, "f": far}
    hop = {"x": 16 * (1 - 2 * x), "y": 8 * (1 - 2 * y), "n": 2 * (1 - 2 * near), "f": 4 * (1 - 2 * far)}
    peer = {d: me + hop[d] for d in hop}

    def quad(hi, lo):
        other_hi, other_lo = 1 - bit[hi], 1 - bit[lo]
        return (
            (2 * bit[hi] + other_lo, peer[lo]),
            (2 * other_hi + bit[lo], peer[hi]),
            (2 * other_hi + other_lo, me + hop[hi] + hop[lo]),
        )

    quads = {"q": quad("f", "n"), "p": quad("x", "y")}
    place_in = {"q": 2 * far + near, "p": 2 * x + y}

    barrier = pltpu.get_barrier_semaphore()
    for device in (partner, *[device for q in quads.values() for _, device in q]):
        pl.semaphore_signal(barrier, inc=1, device_id={"tp": device}, device_id_type=MESH)

    def stream(step, slot):
        rows = pl.ds(pl.multiple_of(step * R, R), R)
        return (
            pltpu.make_async_copy(wg_hbm.at[rows, :], wbuf.at[slot, :, pl.ds(0, FF)], psem.at[0, slot]),
            pltpu.make_async_copy(wu_hbm.at[rows, :], wbuf.at[slot, :, pl.ds(FF, FF)], psem.at[0, slot]),
            pltpu.make_async_copy(x_hbm.at[:, rows], xbuf.at[slot], psem.at[1, slot]),
        )

    def down(t):
        odd = lax.rem(t, 2)
        half = odd * core + (1 - odd) * (1 - core)
        inner = lax.div(t, 2) * T
        src = wd_hbm.at[:, pl.ds(pl.multiple_of(half * HALF + inner, T), T)]
        return pltpu.make_async_copy(src, wd.at[odd, :, pl.ds(pl.multiple_of(inner, T), T)], wsem.at[t])

    def landed(ref, sem):
        pltpu.make_async_copy(ref, ref, sem).wait()

    def project(step):
        slot = lax.rem(step, NS)
        landed(wbuf.at[slot], psem.at[0, slot])
        landed(xbuf.at[slot], psem.at[1, slot])
        acc[...] += jnp.dot(xbuf[slot], wbuf[slot], preferred_element_type=F32)
        return slot

    for i in range(NS):
        for c in stream(i, i):
            c.start()
    acc[...] = jnp.zeros_like(acc)

    @pl.loop(0, STEPS - NS)
    def _(step):
        slot = project(step)
        for c in stream(step + NS, slot):
            c.start()

    @pl.loop(STEPS - NS, STEPS)
    def _(step):
        for i in range(PER):
            down(PER * (step - (STEPS - NS)) + i).start()
        project(step)

    gate, up = acc[:, :FF], acc[:, FF:]
    hid[...] = (jax.nn.silu(gate) * up).astype(BF16)
    pl.semaphore_wait(barrier, 7)

    def start(src, dst, ss, rs, device):
        pltpu.make_async_remote_copy(
            src_ref=src, dst_ref=dst, send_sem=ss, recv_sem=rs, device_id={"tp": device}, device_id_type=MESH
        ).start()

    waited = set()

    def chunk(s):
        width, dims = CHUNKS[s]
        first, m = STARTS[s], len(dims)
        cols = pl.ds(first, width)
        ocols = pl.ds(pl.multiple_of(core * HALF + first, 128), width)
        pcols = pl.ds(pl.multiple_of((1 - core) * HALF + first, 128), width)
        at, sizes = [0], [NB]
        for d in dims:
            if d in quads:
                sizes.append(sizes[-1] // 4)
                at.append(at[-1] + place_in[d] * sizes[-1])
            elif d in bit:
                sizes.append(sizes[-1] // 2)
                at.append(at[-1] + bit[d] * sizes[-1])
            else:
                sizes.append(sizes[-1])
                at.append(at[-1])
        last_gather = m - 1 if dims[-1] in quads or dims[-1] in bit else m - 2

        def targets(j):
            d, size = dims[j], sizes[j + 1]
            if d in quads:
                return [(at[j] + i * size, device) for i, device in quads[d]]
            return [(at[j] + (1 - bit[d]) * size, peer[d])]

        def held(j):
            return [2 * NB - sizes[j] + i * sizes[j + 1] for i in range(3 if dims[j] in quads else 1)]

        def arrived(j):
            if j < 0:
                landed(rbuf.at[pl.ds(0, NB), :, cols], recv_sem.at[s, 0])
            elif dims[j].isupper():
                landed(swap.at[:, :, cols], recv_sem.at[s, j + 1])
            else:
                count = len(held(j)) * sizes[j + 1]
                landed(rbuf.at[pl.ds(held(j)[0], count), :, cols], recv_sem.at[s, j + 1])

        def gathered(j):
            count = (3 if dims[j] in quads else 1) * sizes[j + 1]
            landed(rbuf.at[pl.ds(0, count), :, cols], recv_sem.at[s, j])

        def total(j, begin, count):
            value = own[pl.ds(begin, count), :, cols]
            for base in held(j) if j >= 0 else [0]:
                value += rbuf[pl.ds(base + begin - at[j + 1], count), :, cols].astype(F32)
            return value

        def give(begin, count, device, sem):
            ref = out.at[pl.ds(begin, count), :, ocols]
            start(ref, ref, send_ag.at[s], recv_sem.at[s, sem], device)

        def spread(j):
            for _, device in targets(j):
                give(at[j + 1], sizes[j + 1], device, j)
            if j == 0:
                give(at[1], sizes[1], partner, m + 1)

        def matmul():
            for side in (0, 1):
                for t in range(2 * (first // T) + side, 2 * ((first + width - 1) // T) + side + 1, 2):
                    if t not in waited:
                        waited.add(t)
                        down(t).wait()
                p = jnp.dot(hid[...], wd[side, :, cols], preferred_element_type=F32).reshape(NB, BLK, width)
                if side == 0:
                    span = pl.ds(0, NB)
                    sbuf[span, :, cols] = p.astype(BF16)
                    start(sbuf.at[span, :, cols], rbuf.at[span, :, cols], send_rs.at[s], recv_sem.at[s, 0], partner)
                else:
                    own[:, :, cols] = p

        yield matmul
        for j in range(m):

            def reduce(j=j):
                arrived(j - 1)
                size = sizes[j + 1]
                if dims[j].isupper():
                    span = pl.ds(at[j], size)
                    own[span, :, cols] = total(j - 1, at[j], size)
                    device = peer[dims[j].lower()]
                    start(own.at[span, :, cols], swap.at[:, :, cols], send_swap.at[s], recv_sem.at[s, j + 1], device)
                    return
                for base, (begin, device) in zip(held(j), targets(j), strict=True):
                    span = pl.ds(base, size)
                    sbuf[span, :, cols] = total(j - 1, begin, size).astype(BF16)
                    start(sbuf.at[span, :, cols], rbuf.at[span, :, cols], send_rs.at[s], recv_sem.at[s, j + 1], device)
                own[pl.ds(at[j + 1], size), :, cols] = total(j - 1, at[j + 1], size)

            yield reduce

        def finish():
            arrived(m - 1)
            span = pl.ds(at[m], sizes[m])
            if dims[-1].isupper():
                value = own[span, :, cols] + swap[:, :, cols]
            else:
                value = total(m - 1, at[m], sizes[m])
            out[span, :, ocols] = value.astype(BF16)
            spread(last_gather)

        yield finish
        for j in range(last_gather - 1, -1, -1):

            def gather(j=j):
                gathered(j + 1)
                spread(j)

            yield gather

        def gather_core():
            gathered(0)
            for begin, _ in targets(0):
                give(begin, sizes[1], partner, m + 1)

        yield gather_core

        def done():
            landed(out.at[:, :, pcols], recv_sem.at[s, m + 1])

        yield done

    chunks = [chunk(s) for s in range(S)]
    for s in ORDER:
        task = next(chunks[s])
        with jax.named_scope(f"{task.__name__}_{s}"):
            task()
    for s, (width, dims) in enumerate(CHUNKS):
        cols = pl.ds(STARTS[s], width)
        swaps = dims[-1].isupper()
        sent = sbuf.at[pl.ds(0, 2 * NB - (2 if swaps else 1)), :, cols]
        landed(sent, send_rs.at[s])
        landed(sent, send_ag.at[s])
        if swaps:
            landed(swap.at[:, :, cols], send_swap.at[s])


def block(x, w_gate, w_up, w_down):
    dma = pltpu.SemaphoreType.DMA
    out = pl.pallas_call(
        kernel,
        name="mlp",
        out_shape=pltpu.VMEM((NB, BLK, D), BF16),
        in_specs=[pl.BlockSpec(memory_space=pl.ANY)] * 4,
        out_specs=pl.BlockSpec(memory_space=pltpu.VMEM),
        scratch_shapes=[
            pltpu.VMEM((NS, R, 2 * FF), BF16),
            pltpu.VMEM((NS, ROWS, R), BF16),
            pltpu.VMEM((ROWS, 2 * FF), F32),
            pltpu.VMEM((ROWS, FF), BF16),
            pltpu.VMEM((2, FF, HALF), BF16),
            pltpu.VMEM((NB, BLK, HALF), F32),
            pltpu.VMEM((2 * NB, BLK, HALF), BF16),
            pltpu.VMEM((2 * NB, BLK, HALF), BF16),
            pltpu.VMEM((2, BLK, HALF), F32),
            dma((2, NS)),
            dma((TILES,)),
            dma((S,)),
            dma((S,)),
            dma((S,)),
            dma((S, 2 + max(len(dims) for _, dims in CHUNKS))),
        ],
        compiler_params=pltpu.CompilerParams(
            collective_id=0, has_side_effects=True, vmem_limit_bytes=50 * 1024 * 1024
        ),
        cost_estimate=pl.CostEstimate(flops=6 * ROWS * D * FF, bytes_accessed=6 * D * FF, transcendentals=ROWS * FF),
    )(x, w_gate, w_up, w_down)
    return out.reshape(ROWS, D)


def solution(mesh):
    return jax.shard_map(
        block,
        mesh=mesh,
        in_specs=(P("dp", None), P(None, "tp"), P(None, "tp"), P("tp", None)),
        out_specs=P("dp", None),
        check_vma=False,
    )
```

time: 63.4 us -> 61.2 us (0.965)
  Pallas kernels: 61.6 us -> 59.3 us
    pallas_call x1, Pallas kernels: 61.6 us -> 59.3 us  [block(): pl.pallas_call(kernel, name='mlp', out_shape=pltpu.VMEM((NB, BLK, D), BF1...]
where the time goes in v3:
time: 61.2 us; the launch traced here: 61 us
  Pallas kernels  59.3 us (97%)
  local copies, waits for them, and re-layouts  1.67 us (3%)
    pallas_call x1, Pallas kernels, block(): pl.pallas_call(kernel, name='mlp', out_shape=pltpu.VMEM((NB, BLK, D), BF1...  59.3 us
    unnamed x1, local copies, waits for them, and re-layouts  1.67 us

profile of v3, /device:TPU:0, one launch (start us, length us, event | category | flops | bytes accessed | tf_op | source)
XLA Modules:
  0.0 61.0 jit_solution(9841882054193964349)
XLA Ops:
  0.0 59.3 %mlp.1 = bf16[16,8,12288]{2,1,0:T(8,128)(2,1)S(1)} custom-call(bf16[128,12288]{1,0:T(8,128)(2,1)} %x_hbm.1, bf16[12288,896]{1,0:T(8,128)(2,1)} %wg_hbm.1, bf16[12288,896]{1,0:T(8,128)(2,1)} %wu_hbm.1, bf16[896,12288]{1,0:T(8,128)(2,1)} %wd_hbm.1), custom_call_target="tpu_custom_call" | custom-call | flops 8455716864 | bytes 66060288 | tf_op jit(solution)/shard_map/mlp/pallas_call | solution.py:256
  59.3 1.7 %copy.6 = bf16[128,12288]{1,0:T(8,128)(2,1)} copy(bf16[128,12288]{1,0:T(8,128)(2,1)S(1)} %bitcast.1) | data formatting | bytes 6291456
